TPU v7x, 32 devices: a whole 2x2x4 slice. The times are simulated.
32 devices in a mesh: band: 4 (over z), px: 4 (over x, core), py: 2 (over y).
Axes of the slice: x: 2, y: 2, z: 4, core: 2. Of those that a mesh axis runs over, the one named last changes fastest.
Arguments:
- orbitals: bfloat16 [4, 1024, 384], P('band', ('px', 'py')), may hold values from -0.01171875 to 0.01171875
- occupations: float32 [4], P('band'), may hold values from 0.2 to 2
- stick_map: int32 [2, 1024], P(None, 'px'), may hold values from 0 to 191, as said below
- core_density: float32 [192, 192, 192], P('py', 'px'), may hold values from 0.05 to 0.5
Outputs:
- potential: float32 [192, 192, 192], P('py', 'px')
- gradient: float32 [3, 192, 192, 192], P(None, 'py', 'px')
Inputs may be any that keep to these rules, and one draw needn't show every extreme that they name: `stick_map`: columns i * 128 * 2 to (i + 1) * 128 * 2 - 1 have x index from i * 48 to (i + 1) * 48 - 1; no two columns share a grid position.
All inputs are finite; a program needn't handle non-finite values.
Results may differ from a plain program's by a relative error of at most 0.0054.
Values may be sent and summed in bfloat16 or wider, within the bound.
No kernel may reach another device: no remote copies, remote signals or barrier semaphores. Data moves between devices by JAX's collectives and lax.ppermute only.
A program may use at most 128 MiB of HBM per device.

v0:
```python
import math
import jax
import jax.numpy as jnp
from jax import lax
from jax.sharding import PartitionSpec as P

SPACING = 0.25
PBE_KAPPA = 0.804
PBE_MU = 0.2195
SLATER_COEF = 0.75 * (3.0 / math.pi) ** (1.0 / 3.0)
REDUCED_SCALE = 4.0 * (3.0 * math.pi**2) ** (2.0 / 3.0)
HIGHEST_PREC = lax.Precision.HIGHEST


def complex_table(row_index, col_index, points, direction):
    product = row_index[:, None] * col_index[None, :] % points
    angles = 2.0 * math.pi / points * product.astype(jnp.float32)
    cosine = jnp.cos(angles)
    sine_part = direction * jnp.sin(angles)
    return jnp.stack([jnp.stack([cosine, sine_part], 1), jnp.stack([-sine_part, cosine], 1)], 0)


def freq_pair(positions, points):
    signed = jnp.where(positions <= points // 2, positions, positions - points).astype(jnp.float32)
    gradient_freq = jnp.where(positions == points // 2, 0.0, signed)
    return (signed, gradient_freq)


def swap_rows(values):
    return lax.all_to_all(values, "px", split_axis=1, concat_axis=0, tiled=True)


def swap_depth(values):
    moved = lax.all_to_all(values, ("band", "py"), split_axis=1, concat_axis=0, tiled=True)
    return moved


def exchange_part(density, fields):
    cube_root = jnp.cbrt(density)
    four_thirds = density * cube_root
    grad_square = fields[1] * fields[1] + fields[2] * fields[2] + fields[3] * fields[3]
    reduced = grad_square / (REDUCED_SCALE * four_thirds * four_thirds)
    denominator = 1.0 + PBE_MU * reduced / PBE_KAPPA
    enhance = 1.0 + PBE_KAPPA - PBE_KAPPA / denominator
    enhance_slope = PBE_MU / (denominator * denominator)
    potential = fields[0] - SLATER_COEF * cube_root * (
        4.0 / 3.0 * enhance - 8.0 / 3.0 * reduced * enhance_slope
    )
    return jnp.concatenate([potential[None], fields[1:]], 0)


def transform(rho_local, pieces, depth_index, px_index):
    zshare, y_rows, points = rho_local.shape
    rows_px = lax.axis_size("px")
    rows_py = lax.axis_size("py")
    xblock = points // rows_px
    kyblock = points // pieces
    zblock = zshare * (pieces // rows_py)
    every_index = jnp.arange(points, dtype=jnp.int32)
    forward = complex_table(every_index, every_index, points, -1.0)
    x_table = forward[0].reshape(points, 2, rows_px, xblock).transpose(0, 2, 1, 3)
    section_data = jnp.einsum("zyx,xbsk->ybzsk", rho_local, x_table, precision=HIGHEST_PREC)
    section_data = swap_rows(section_data.reshape(y_rows, rows_px, zshare * 2 * xblock))
    section_data = section_data.reshape(points, zshare, 2, xblock)
    y_table = forward.reshape(2, points, 2, pieces, kyblock)
    section_data = jnp.einsum("yzrx,rysdk->zdksx", section_data, y_table, precision=HIGHEST_PREC)
    section_data = swap_depth(section_data.reshape(zshare, pieces, kyblock * 2 * xblock))
    section_data = section_data.reshape(pieces * zshare, kyblock, 2, xblock)
    source = jnp.arange(pieces * zshare, dtype=jnp.int32)
    device = source // zshare
    within = source % zshare
    z_order = device % rows_py * zblock + device // rows_py * zshare + within
    z_table = complex_table(z_order, every_index, points, -1.0)
    spectrum = jnp.einsum("zyrx,rzsk->kysx", section_data, z_table, precision=HIGHEST_PREC)
    q_depth, g_depth = freq_pair(every_index, points)
    ky_index = depth_index * kyblock + jnp.arange(kyblock, dtype=jnp.int32)
    q_col, g_col = freq_pair(ky_index, points)
    kx_index = px_index * xblock + jnp.arange(xblock, dtype=jnp.int32)
    q_row, g_row = freq_pair(kx_index, points)
    wave_unit = 2.0 * math.pi / (points * SPACING)
    squared = wave_unit**2 * (
        q_depth[:, None, None] ** 2 + q_col[None, :, None] ** 2 + q_row[None, None, :] ** 2
    )
    hartree = jnp.where(squared > 0, 4.0 * math.pi / jnp.where(squared > 0, squared, 1.0), 0.0)
    wave_z = wave_unit * g_depth[:, None, None]
    wave_y = wave_unit * g_col[None, :, None]
    wave_x = wave_unit * g_row[None, None, :]
    real_part = spectrum[:, :, 0, :]
    imag_part = spectrum[:, :, 1, :]
    first_factor = hartree - wave_x
    packed = jnp.stack(
        [
            jnp.stack([first_factor * real_part, first_factor * imag_part], 2),
            jnp.stack(
                [-wave_z * real_part - wave_y * imag_part, wave_y * real_part - wave_z * imag_part],
                2,
            ),
        ],
        0,
    )
    inverse = complex_table(every_index, every_index, points, 1.0)
    zi_table = complex_table(every_index, z_order, points, 1.0).reshape(
        2, points, 2, pieces, zshare
    )
    section_data = jnp.einsum("fkyrx,rksdz->ydfzsx", packed, zi_table, precision=HIGHEST_PREC)
    section_data = swap_depth(section_data.reshape(kyblock, pieces, 2 * zshare * 2 * xblock))
    section_data = section_data.reshape(points, 2, zshare, 2, xblock)
    yi_table = inverse.reshape(2, points, 2, rows_px, y_rows)
    section_data = jnp.einsum("kfzrx,rksby->xbfzsy", section_data, yi_table, precision=HIGHEST_PREC)
    section_data = swap_rows(section_data.reshape(xblock, rows_px, 2 * zshare * 2 * y_rows))
    section_data = section_data.reshape(points, 2, zshare, 2, y_rows)
    fields = jnp.einsum("kfzry,rksx->fszyx", section_data, inverse, precision=HIGHEST_PREC)
    fields = fields * (1.0 / float(points) ** 3)
    return fields.reshape(4, zshare, y_rows, points)


def body(orbitals, occupations, stick_map, core_density):
    bands_here, columns_here, doubled = orbitals.shape
    points = doubled // 2
    rows_px = lax.axis_size("px")
    rows_py = lax.axis_size("py")
    groups = lax.axis_size("band")
    px_index = lax.axis_index("px")
    py_index = lax.axis_index("py")
    xblock = points // rows_px
    zblock = points // rows_py
    y_rows = points // rows_px
    every_index = jnp.arange(points, dtype=jnp.int32)
    inverse = complex_table(every_index, every_index, points, 1.0)
    z_table = (
        inverse.reshape(2, points, 2, rows_py, zblock)
        .transpose(0, 1, 3, 2, 4)
        .reshape(doubled, doubled)
    )
    columns = jnp.dot(
        orbitals.astype(jnp.float32).reshape(bands_here * columns_here, doubled),
        z_table,
        precision=HIGHEST_PREC,
    )
    columns = columns.astype(jnp.bfloat16).reshape(bands_here, columns_here, doubled)
    columns = lax.all_to_all(columns, "py", split_axis=2, concat_axis=1, tiled=True)
    slot_index = stick_map[1] * xblock + (stick_map[0] - px_index * xblock)
    plane_data = (
        jnp.zeros((bands_here, points * xblock, 2 * zblock), jnp.float32)
        .at[:, slot_index]
        .set(columns.astype(jnp.float32))
    )
    plane_data = plane_data.reshape(bands_here, points, xblock, 2, zblock)
    plane_data = jnp.einsum("byxrz,rysk->bkxsz", plane_data, inverse, precision=HIGHEST_PREC)
    plane_data = plane_data.astype(jnp.bfloat16).reshape(bands_here, points, xblock * 2 * zblock)
    plane_data = lax.all_to_all(plane_data, "px", split_axis=1, concat_axis=2, tiled=True)
    plane_data = plane_data.astype(jnp.float32).reshape(bands_here, y_rows, points, 2, zblock)
    orbital_values = jnp.einsum("byxrz,rxsk->bszyk", plane_data, inverse, precision=HIGHEST_PREC)
    density = jnp.einsum(
        "b,bszyk->zyk", occupations, orbital_values * orbital_values, precision=HIGHEST_PREC
    )
    zshare = zblock // groups
    band_index = lax.axis_index("band")
    shared_rows = lax.psum_scatter(density, "band", scatter_dimension=0, tiled=True)
    core_rows = lax.dynamic_slice_in_dim(core_density, band_index * zshare, zshare, 0)
    rho_local = shared_rows + core_rows
    fields = transform(rho_local, groups * rows_py, band_index * rows_py + py_index, px_index)
    results = lax.all_gather(exchange_part(rho_local, fields), "band", axis=1, tiled=True)
    return (results[0], results[1:4])


def solution(mesh):
    return jax.shard_map(
        body,
        mesh=mesh,
        in_specs=(P("band", ("px", "py"), None), P("band"), P(None, "px"), P("py", "px", None)),
        out_specs=(P("py", "px", None), P(None, "py", "px", None)),
        check_vma=False,
    )
```

profile of v0, /device:TPU:0, one launch (start us, length us, event | category | flops | bytes accessed | tf_op | source)
XLA Modules:
  0.0 1160.9 jit_solution(13728535052132577211)
XLA Ops:
  7.2 0.8 fusion.90
  10.8 1.2 reduce.3
  12.6 4.3 all-to-all-start
  16.9 0.8 fusion.121
  17.7 0.8 fusion.111
  18.6 2.7 all-to-all-done
  21.9 5.9 scatter_custom_fusion
  27.8 12.3 %reshape.807 = f32[192,48,2,96]{3,2,1,0:T(2,128)} reshape(f32[9216,192]{1,0:T(8,128)} %scatter_custom_fusion) | data formatting | bytes 14155776 | tf_op jit(solution)/shard_map/reshape.2
  40.1 14.2 %copy.140 = f32[192,48,2,96]{0,3,2,1:T(8,128)} copy(f32[192,48,2,96]{3,2,1,0:T(2,128)} %reshape.807) | data formatting | bytes 14155776 | tf_op jit(solution)/shard_map/reshape.2
  54.3 18.6 %fusion.5 = bf16[1,192,48,2,96]{1,4,2,3,0:T(8,128)(2,1)} fusion(f32[192,48,2,96]{0,3,2,1:T(8,128)} %copy.140, f32[1,192,2,192]{3,1,0,2:T(8,128)S(1)} %get-tuple-element.11, f32[1,192,2,192]{3,1,0,2:T(8,128)S(1)} %get-tuple-element.10), kind=kOutput, calls=%fused_computation.8 | convolution fusion | flops 8155643904 | bytes 11206656 | tf_op jit(solution)/shard_map/byxrz,rysk->bkxsz/dot_general | solution.py:149
  72.8 11.6 copy.141
  84.4 24.4 %reshape.857 = bf16[1,192,9216]{2,0,1:T(2,128)(2,1)} reshape(bf16[1,192,48,2,96]{4,3,2,1,0:T(2,128)(2,1)} %copy.141) | data formatting | bytes 7077888 | tf_op jit(solution)/shard_map/reshape | solution.py:150
  108.8 78.5 %reduce.4 = bf16[192,9216]{1,0:T(8,128)(2,1)} reduce(bf16[192,1,9216]{2,1,0:T(2,128)(2,1)} %bitcast.221, bf16[]{:T(256)} %broadcast.1309), dimensions={1}, to_apply=%bitcast.207.reduce_sub_computation | reduce | bytes 7077890
  187.3 5.6 reshape.864
  192.9 4.7 all-to-all-start.1
  198.3 40.5 %all-to-all-done.1 = bf16[4,2,221184]{2,1,0:T(2,128)(2,1)} async-done(((bf16[4,2,221184]{2,1,0:T(2,128)(2,1)}), bf16[4,2,221184]{2,1,0:T(2,128)(2,1)}, u32[]{:S(2)}, u32[]{:S(2)}) %all-to-all-start.1) | async-done | bytes 3538976 | tf_op jit(solution)/shard_map/all_to_all | solution.py:151
  238.8 6.6 reshape.865
  245.4 4.1 copy.194
  249.5 4.5 copy.143
  254.0 14.9 %reshape.809 = bf16[48,192,2,96]{3,2,1,0:T(2,128)(2,1)} reshape(bf16[1,48,4,9216]{3,2,1,0:T(4,128)(2,1)} %copy.143) | data formatting | bytes 7077888 | tf_op jit(solution)/shard_map/reshape.5
  268.9 10.5 fusion.2
  279.5 2.5 multiply_bitcast_fusion
  282.0 6.8 copy.146
  288.8 0.9 fusion.94
  289.7 84.4 %reduce-scatter.2.cloned.1.call-done = f32[24,48,192]{2,1,0:T(8,128)} async-done(((f32[96,48,192]{2,1,0:T(8,128)}), f32[24,48,192]{2,1,0:T(8,128)}) %reduce-scatter.2.cloned.1.call-update) | async-done | bytes 884752 | tf_op jit(solution)/shard_map/reduce_scatter | solution.py:159
  374.1 6.7 convolution_bitcast_fusion
  380.9 7.5 copy.147
  388.4 9.3 reshape.811
  397.7 3.8 all-to-all-start.2
  401.5 0.9 sine_multiply_fusion.1
  402.4 21.2 %all-to-all-done.2 = f32[48,4,2304]{2,0,1:T(8,128)S(1)} async-done(((f32[48,4,2304]{2,0,1:T(8,128)}), f32[48,4,2304]{2,0,1:T(8,128)S(1)}, u32[]{:S(2)}, u32[]{:S(2)}) %all-to-all-start.2) | async-done | bytes 1769504 | tf_op jit(solution)/shard_map/all_to_all | solution.py:30
  423.6 8.6 reshape.812
  432.2 10.4 fusion.27
  442.6 5.8 copy.186
  448.4 9.7 reshape.858
  458.1 5.1 all-to-all-start.3
  463.3 0.9 sine_multiply_fusion.2
  464.2 0.9 maximum_bitcast_fusion.14
  465.2 1.6 fusion.103
  466.9 37.3 %all-to-all-done.3 = f32[24,8,2304]{2,0,1:T(8,128)S(1)} async-done(((f32[24,8,2304]{2,0,1:T(8,128)}), f32[24,8,2304]{2,0,1:T(8,128)S(1)}, u32[]{:S(2)}, u32[]{:S(2)}) %all-to-all-start.3) | async-done | bytes 1769504 | tf_op jit(solution)/shard_map/all_to_all | solution.py:34
  504.1 8.6 reshape.814
  512.7 5.7 copy.152
  518.4 5.1 fusion.34
  523.6 0.8 slice_multiply_fusion.4
  525.6 15.9 %fusion.22 = f32[24,8,2,24,2,48]{5,3,0,2,1,4:T(8,128)S(1)} fusion(f32[1,192,24,2,48]{1,4,2,3,0:T(8,128)S(1)} %maximum_bitcast_fusion.5, f32[1,192,24,2,48]{1,4,2,3,0:T(8,128)S(1)} %maximum_bitcast_fusion.4, f32[1,192,1,8,24]{1,4,0,3,2:T(8,128)S(1)} %copy-done.4, f32[1,192,1,8,24]{1,4,0,3,2:T(8,128)S(1)} %copy-done.3, ...), kind=kOutput, calls=%fused_computation.28 | convolution fusion | flops 4078190592 | bytes 7520256 | tf_op jit(solution)/shard_map/fkyrx,rksdz->ydfzsx/dot_general | solution.py:105
  541.5 8.0 copy.189
  549.5 16.6 %reshape.859 = f32[24,8,4608]{2,0,1:T(8,128)} reshape(f32[24,8,2,24,2,48]{5,4,3,2,0,1:T(2,128)} %copy.189) | data formatting | bytes 7077888 | tf_op jit(solution)/shard_map/reshape | solution.py:106
  566.1 4.5 all-to-all-start.4
  570.6 0.9 fusion.107
  571.5 77.6 %all-to-all-done.4 = f32[24,8,4608]{2,0,1:T(8,128)} async-done(((f32[24,8,4608]{2,0,1:T(8,128)}), f32[24,8,4608]{2,0,1:T(8,128)}, u32[]{:S(2)}, u32[]{:S(2)}) %all-to-all-start.4) | async-done | bytes 3538976 | tf_op jit(solution)/shard_map/all_to_all | solution.py:34
  649.2 17.3 %reshape.816 = f32[192,2,24,2,48]{4,3,2,1,0:T(2,128)} reshape(f32[8,24,1,4608]{3,1,0,2:T(8,128)} %bitcast.63) | data formatting | bytes 7077888 | tf_op jit(solution)/shard_map/reshape | solution.py:107
  666.5 24.9 %fusion.19 = f32[48,4,2,24,2,48]{0,5,3,2,1,4:T(8,128)} fusion(f32[192,2,24,2,48,1,1]{4,3,2,1,0,6,5:T(2,128)} %bitcast.218, f32[1,192,1,4,48]{1,4,0,3,2:T(8,128)S(1)} %get-tuple-element.20, f32[1,192,1,4,48]{1,4,0,3,2:T(8,128)S(1)} %get-tuple-element.19, f32[1,192,1,4,48]{1,4,0,3,2:T(8,128)S(1)} %get-tuple-element.18), kind=kOutput, calls=%fused_computation.27 | convolution fusion | flops 4077305856 | bytes 7520256 | tf_op jit(solution)/shard_map/kfzrx,rksby->xbfzsy/dot_general | solution.py:109
  691.4 13.7 %copy.157 = f32[48,4,2,24,2,48]{5,4,3,2,0,1:T(2,128)} copy(f32[48,4,2,24,2,48]{0,5,3,2,1,4:T(8,128)} %fusion.19) | data formatting | bytes 7077888 | tf_op jit(solution)/shard_map/kfzrx,rksby->xbfzsy/transpose | solution.py:109
  705.1 16.6 %reshape.817 = f32[48,4,4608]{2,0,1:T(8,128)} reshape(f32[48,4,2,24,2,48]{5,4,3,2,0,1:T(2,128)} %copy.157) | data formatting | bytes 7077888 | tf_op jit(solution)/shard_map/reshape | solution.py:110
  721.7 46.9 %all_to_all.84 = f32[48,4,4608]{2,0,1:T(8,128)} all-to-all(f32[48,4,4608]{2,0,1:T(8,128)} %reshape.817), channel_id=1, replica_groups=mesh['band'=4,'px'=4,'py'=2] {'px'}, dimensions={1} | all-to-all | bytes 7077888 | tf_op jit(solution)/shard_map/all_to_all | solution.py:30
  768.6 17.1 %reshape.818 = f32[192,2,24,2,48]{4,3,2,1,0:T(2,128)} reshape(f32[4,48,1,4608]{3,1,0,2:T(8,128)} %bitcast.224) | data formatting | bytes 7077888 | tf_op jit(solution)/shard_map/reshape | solution.py:111
  785.7 13.2 %copy.158 = f32[192,2,24,2,48]{0,4,3,2,1:T(8,128)} copy(f32[192,2,24,2,48]{4,3,2,1,0:T(2,128)} %reshape.818) | data formatting | bytes 7077888 | tf_op jit(solution)/shard_map/reshape | solution.py:111
  798.9 10.3 fusion.9
  809.8 1.0 copy-done.2
  810.8 3.1 fusion.41
  814.0 2.6 pad_maximum_fusion
  816.6 320.4 %all-gather.2.cloned.1.call-done = f32[4,96,48,192]{3,2,1,0:T(8,128)} async-done(((f32[4,24,48,192]{3,2,1,0:T(8,128)}), f32[4,96,48,192]{3,2,1,0:T(8,128)}) %all-gather.2.cloned.1.call-update) | async-done | bytes 14155792 | tf_op jit(solution)/shard_map/all_gather | solution.py:163
  1137.0 4.8 slice_bitcast_fusion
  1141.8 11.8 %slice.55 = f32[3,96,48,192]{3,2,1,0:T(8,128)} slice(f32[4,96,48,192]{3,2,1,0:T(8,128)} %all-gather.2.cloned.1.call-done), slice={[1:4], [0:96], [0:48], [0:192]} | slice | bytes 21233664 | tf_op jit(solution)/shard_map/slice | solution.py:164
  (42 shorter events, 6.1 us)
Async XLA Ops:
  7.2 2.2 copy-start
  8.1 10.4 copy-start.5
  12.6 8.6 all-to-all-start
  192.9 45.9 %all-to-all-start.1 = ((bf16[4,2,221184]{2,1,0:T(2,128)(2,1)}), bf16[4,2,221184]{2,1,0:T(2,128)(2,1)}, u32[]{:S(2)}, u32[]{:S(2)}) async-start(bf16[4,2,221184]{2,1,0:T(2,128)(2,1)} %reshape.864), calls=%async_computation.1 | async-start | bytes 7077888 | tf_op jit(solution)/shard_map/all_to_all | solution.py:151
  197.6 176.5 %reduce-scatter.2.cloned.1.call-start = ((), (), s32[]{:S(2)}) async-start(), calls=%async_computation.7 | async-start | bytes 5898240 | tf_op jit(solution)/shard_map/reduce_scatter | solution.py:159
  397.7 25.9 %all-to-all-start.2 = ((f32[48,4,2304]{2,0,1:T(8,128)}), f32[48,4,2304]{2,0,1:T(8,128)S(1)}, u32[]{:S(2)}, u32[]{:S(2)}) async-start(f32[48,4,2304]{2,0,1:T(8,128)} %reshape.811), calls=%async_computation.3 | async-start | bytes 3538944 | tf_op jit(solution)/shard_map/all_to_all | solution.py:30
  458.1 46.0 %all-to-all-start.3 = ((f32[24,8,2304]{2,0,1:T(8,128)}), f32[24,8,2304]{2,0,1:T(8,128)S(1)}, u32[]{:S(2)}, u32[]{:S(2)}) async-start(f32[24,8,2304]{2,0,1:T(8,128)} %reshape.858), calls=%async_computation.4 | async-start | bytes 3538944 | tf_op jit(solution)/shard_map/all_to_all | solution.py:34
  524.6 0.9 copy-start.3
  524.6 1.0 copy-start.4
  566.1 83.1 %all-to-all-start.4 = ((f32[24,8,4608]{2,0,1:T(8,128)}), f32[24,8,4608]{2,0,1:T(8,128)}, u32[]{:S(2)}, u32[]{:S(2)}) async-start(f32[24,8,4608]{2,0,1:T(8,128)} %reshape.859), calls=%async_computation.5 | async-start | bytes 7077888 | tf_op jit(solution)/shard_map/all_to_all | solution.py:34
  570.6 566.4 %all-gather.2.cloned.1.call-start = ((), (), s32[]{:S(2)}) async-start(), calls=%async_computation.8 | async-start | bytes 23592960 | tf_op jit(solution)/shard_map/all_gather | solution.py:163
  809.6 1.3 copy-start.2
  1141.8 11.8 %copy-start.1 = (bf16[1,128,384]{2,1,0:T(8,128)(2,1)S(1)}, bf16[1,128,384]{2,1,0:T(8,128)(2,1)}, u32[]{:S(2)}) copy-start(bf16[1,128,384]{2,1,0:T(8,128)(2,1)} %param.4) | copy-start | bytes 294916
Sparse Core Ops, SparseCore 0:
  288.9 85.1 reduce-scatter.1
  816.7 320.2 all-gather.1
where the time goes:
time: 1170 us; the launch traced here: 1160 us
  waiting for transfers between devices  584 us (50%)
  local copies, waits for them, and re-layouts  291 us (25%)
  matrix products  103 us (9%)
  other arithmetic  98.1 us (8%)
  blocking collectives  46.9 us (4%)
  starting transfers between devices  22.4 us (2%)
  between operations  15.5 us (1%)
    all_gather x1, waiting for transfers between devices, body(): lax.all_gather(exchange_part(rho_local, fields), 'band', axis=1, tiled=True)  320 us
    all_to_all x2, waiting for transfers between devices, swap_depth(): lax.all_to_all(values, ('band', 'py'), split_axis=1, concat_axis=0, tiled...  115 us
    reduce_scatter x1, waiting for transfers between devices, body(): lax.psum_scatter(density, 'band', scatter_dimension=0, tiled=True)  84.4 us
    unnamed x2, other arithmetic  79.7 us
    all_to_all x1, blocking collectives, swap_rows(): return lax.all_to_all(values, 'px', split_axis=1, concat_axis=0, tiled=True)  46.9 us
    another operation x3, local copies, waits for them, and re-layouts  41.4 us
    all_to_all x1, waiting for transfers between devices, body(): lax.all_to_all(plane_data, 'px', split_axis=1, concat_axis=2, tiled=True)  40.5 us
    reshape x2, local copies, waits for them, and re-layouts, transform(): section_data = section_data.reshape(points, 2, zshare, 2, y_rows)  30.3 us
  transfers between devices with their start and end apart: 7, of which 7 were waited for; matrix products, arithmetic and copies ran while one was open for 1% of the time, Pallas kernels for 0%

commit v1 on v0

--- a/solution.py
+++ b/solution.py
@@ -27,7 +27,16 @@
 
 
 def swap_rows(values):
-    return lax.all_to_all(values, "px", split_axis=1, concat_axis=0, tiled=True)
+
+    def _number_regions(frame_in, dim_k, out_dim):
+        mat_out = lax.axis_size("px")
+        r1 = jnp.split(frame_in, mat_out, axis=dim_k)
+        row_out = jnp.stack(r1)
+        part_now = lax.all_to_all(row_out, axis_name="px", split_axis=0, concat_axis=0)
+        u_next = jnp.concatenate(part_now, axis=out_dim)
+        return u_next
+
+    return _number_regions(values, 1, 0)
 
 
 def swap_depth(values):

time: 1170 us -> 1170 us (level)
    another operation x3 -> x8, local copies, waits for them, and re-layouts: 41.4 us -> 82.6 us
    reshape x3 -> x0, local copies, waits for them, and re-layouts: 38.8 us -> none  [the longest x2 30.3 us: transform(): section_data = section_data.reshape(points, 2, zshare, 2, y_rows)]
where the time goes in v1:
time: 1170 us; the launch traced here: 1160 us
  waiting for transfers between devices  584 us (50%)
  local copies, waits for them, and re-layouts  292 us (25%)
  matrix products  103 us (9%)
  other arithmetic  99.6 us (9%)
  blocking collectives  44.7 us (4%)
  starting transfers between devices  22.4 us (2%)
  between operations  15.5 us (1%)
    all_gather x1, waiting for transfers between devices, body(): lax.all_gather(exchange_part(rho_local, fields), 'band', axis=1, tiled=True)  320 us
    all_to_all x2, waiting for transfers between devices, swap_depth(): lax.all_to_all(values, ('band', 'py'), split_axis=1, concat_axis=0, tiled...  115 us
    reduce_scatter x1, waiting for transfers between devices, body(): lax.psum_scatter(density, 'band', scatter_dimension=0, tiled=True)  84.4 us
    unnamed x2, other arithmetic  79.6 us
    all_to_all x1, blocking collectives, _number_regions(): lax.all_to_all(row_out, axis_name='px', split_axis=0, concat_axis=0)  44.7 us
    another operation x3, local copies, waits for them, and re-layouts  41.4 us
    all_to_all x1, waiting for transfers between devices, body(): lax.all_to_all(plane_data, 'px', split_axis=1, concat_axis=2, tiled=True)  40.5 us
    another operation x2, local copies, waits for them, and re-layouts, transform(): section_data = section_data.reshape(points, 2, zshare, 2, y_rows)  30.3 us
  transfers between devices with their start and end apart: 7, of which 7 were waited for; matrix products, arithmetic and copies ran while one was open for 1% of the time, Pallas kernels for 0%

profile of v1, /device:TPU:0, one launch (start us, length us, event | category | flops | bytes accessed | tf_op | source)
XLA Modules:
  0.0 1161.8 jit_solution(7209765380261062271)
XLA Ops:
  7.2 0.8 fusion.90
  10.8 1.1 reduce.3
  12.6 4.3 all-to-all-start
  18.5 2.7 all-to-all-done
  21.8 5.9 scatter_custom_fusion
  27.7 12.3 %reshape.799 = f32[192,48,2,96]{3,2,1,0:T(2,128)} reshape(f32[9216,192]{1,0:T(8,128)} %scatter_custom_fusion) | data formatting | bytes 14155776 | tf_op jit(solution)/shard_map/reshape.2
  40.0 14.2 %copy.146 = f32[192,48,2,96]{0,3,2,1:T(8,128)} copy(f32[192,48,2,96]{3,2,1,0:T(2,128)} %reshape.799) | data formatting | bytes 14155776 | tf_op jit(solution)/shard_map/reshape.2
  54.2 18.6 %fusion.5 = bf16[1,192,48,2,96]{1,4,2,3,0:T(8,128)(2,1)} fusion(f32[192,48,2,96]{0,3,2,1:T(8,128)} %copy.146, f32[1,192,2,192]{3,1,0,2:T(8,128)S(1)} %get-tuple-element.19, f32[1,192,2,192]{3,1,0,2:T(8,128)S(1)} %get-tuple-element.18), kind=kOutput, calls=%fused_computation.8 | convolution fusion | flops 8155643904 | bytes 11206656 | tf_op jit(solution)/shard_map/byxrz,rysk->bkxsz/dot_general | solution.py:158
  72.8 11.6 %copy.147 = bf16[1,192,48,2,96]{4,3,2,1,0:T(2,128)(2,1)} copy(bf16[1,192,48,2,96]{1,4,2,3,0:T(8,128)(2,1)} %fusion.5) | data formatting | bytes 7077888 | tf_op jit(solution)/shard_map/convert_element_type | solution.py:159
  84.4 24.4 %reshape.847 = bf16[1,192,9216]{2,0,1:T(2,128)(2,1)} reshape(bf16[1,192,48,2,96]{4,3,2,1,0:T(2,128)(2,1)} %copy.147) | data formatting | bytes 7077888 | tf_op jit(solution)/shard_map/reshape | solution.py:159
  108.8 78.5 %reduce.4 = bf16[192,9216]{1,0:T(8,128)(2,1)} reduce(bf16[192,1,9216]{2,1,0:T(2,128)(2,1)} %bitcast.231, bf16[]{:T(256)} %broadcast.1309), dimensions={1}, to_apply=%bitcast.217.reduce_sub_computation | reduce | bytes 7077890
  187.3 5.6 reshape.854
  192.8 4.7 all-to-all-start.1
  198.3 40.5 %all-to-all-done.1 = bf16[4,2,221184]{2,1,0:T(2,128)(2,1)} async-done(((bf16[4,2,221184]{2,1,0:T(2,128)(2,1)}), bf16[4,2,221184]{2,1,0:T(2,128)(2,1)}, u32[]{:S(2)}, u32[]{:S(2)}) %all-to-all-start.1) | async-done | bytes 3538976 | tf_op jit(solution)/shard_map/all_to_all | solution.py:160
  238.8 6.6 reshape.855
  245.4 4.1 copy.200
  249.5 4.5 copy.149
  254.0 14.9 %reshape.801 = bf16[48,192,2,96]{3,2,1,0:T(2,128)(2,1)} reshape(bf16[1,48,4,9216]{3,2,1,0:T(4,128)(2,1)} %copy.149) | data formatting | bytes 7077888 | tf_op jit(solution)/shard_map/reshape.5
  268.9 10.5 fusion.2
  279.4 2.5 multiply_bitcast_fusion
  281.9 6.8 copy.152
  288.8 0.9 fusion.94
  289.7 84.4 %reduce-scatter.2.cloned.1.call-done = f32[24,48,192]{2,1,0:T(8,128)} async-done(((f32[96,48,192]{2,1,0:T(8,128)}), f32[24,48,192]{2,1,0:T(8,128)}) %reduce-scatter.2.cloned.1.call-update) | async-done | bytes 884752 | tf_op jit(solution)/shard_map/reduce_scatter | solution.py:168
  374.1 6.7 convolution_bitcast_fusion
  380.8 7.5 copy.153
  388.4 8.5 reshape.803
  397.0 1.3 pad_maximum_fusion.2
  398.3 3.8 all-to-all-start.2
  402.1 0.9 sine_multiply_fusion.1
  403.0 21.2 %all-to-all-done.2 = f32[4,48,1,2304]{3,1,2,0:T(8,128)S(1)} async-done(((f32[4,48,1,2304]{3,1,2,0:T(8,128)}), f32[4,48,1,2304]{3,1,2,0:T(8,128)S(1)}, u32[]{:S(2)}, u32[]{:S(2)}) %all-to-all-start.2) | async-done | bytes 1769504 | tf_op jit(solution)/shard_map/all_to_all | solution.py:35
  424.2 8.6 reshape_reshape.6
  432.8 10.4 fusion.27
  443.2 5.8 copy.192
  449.0 9.7 reshape.848
  458.7 5.1 all-to-all-start.3
  463.9 0.9 sine_multiply_fusion.2
  464.8 1.0 maximum_bitcast_fusion.14
  465.8 1.6 fusion.103
  467.5 37.2 %all-to-all-done.3 = f32[24,8,2304]{2,0,1:T(8,128)S(1)} async-done(((f32[24,8,2304]{2,0,1:T(8,128)}), f32[24,8,2304]{2,0,1:T(8,128)S(1)}, u32[]{:S(2)}, u32[]{:S(2)}) %all-to-all-start.3) | async-done | bytes 1769504 | tf_op jit(solution)/shard_map/all_to_all | solution.py:43
  504.7 8.6 reshape.805
  513.3 5.7 copy.158
  519.0 5.1 fusion.34
  524.2 0.8 slice_multiply_fusion.4
  526.2 15.9 %fusion.22 = f32[24,8,2,24,2,48]{5,3,0,2,1,4:T(8,128)S(1)} fusion(f32[1,192,24,2,48]{1,4,2,3,0:T(8,128)S(1)} %maximum_bitcast_fusion.5, f32[1,192,24,2,48]{1,4,2,3,0:T(8,128)S(1)} %maximum_bitcast_fusion.4, f32[1,192,1,8,24]{1,4,0,3,2:T(8,128)S(1)} %copy-done.4, f32[1,192,1,8,24]{1,4,0,3,2:T(8,128)S(1)} %copy-done.3, ...), kind=kOutput, calls=%fused_computation.29 | convolution fusion | flops 4078190592 | bytes 7520256 | tf_op jit(solution)/shard_map/fkyrx,rksdz->ydfzsx/dot_general | solution.py:114
  542.1 8.0 copy.195
  550.1 16.6 %reshape.849 = f32[24,8,4608]{2,0,1:T(8,128)} reshape(f32[24,8,2,24,2,48]{5,4,3,2,0,1:T(2,128)} %copy.195) | data formatting | bytes 7077888 | tf_op jit(solution)/shard_map/reshape | solution.py:115
  566.7 4.5 all-to-all-start.4
  571.2 0.9 fusion.107
  572.1 77.6 %all-to-all-done.4 = f32[24,8,4608]{2,0,1:T(8,128)} async-done(((f32[24,8,4608]{2,0,1:T(8,128)}), f32[24,8,4608]{2,0,1:T(8,128)}, u32[]{:S(2)}, u32[]{:S(2)}) %all-to-all-start.4) | async-done | bytes 3538976 | tf_op jit(solution)/shard_map/all_to_all | solution.py:43
  649.8 17.3 %reshape.807 = f32[192,2,24,2,48]{4,3,2,1,0:T(2,128)} reshape(f32[8,24,1,4608]{3,1,0,2:T(8,128)} %bitcast.65) | data formatting | bytes 7077888 | tf_op jit(solution)/shard_map/reshape | solution.py:116
  667.1 24.9 %fusion.19 = f32[48,4,2,24,2,48]{0,5,3,2,1,4:T(8,128)} fusion(f32[192,2,24,2,48,1,1]{4,3,2,1,0,6,5:T(2,128)} %bitcast.228, f32[1,192,1,4,48]{1,4,0,3,2:T(8,128)S(1)} %get-tuple-element.28, f32[1,192,1,4,48]{1,4,0,3,2:T(8,128)S(1)} %get-tuple-element.27, f32[1,192,1,4,48]{1,4,0,3,2:T(8,128)S(1)} %get-tuple-element.26), kind=kOutput, calls=%fused_computation.28 | convolution fusion | flops 4077305856 | bytes 7520256 | tf_op jit(solution)/shard_map/kfzrx,rksby->xbfzsy/dot_general | solution.py:118
  691.9 13.7 %copy.163 = f32[48,4,2,24,2,48]{5,4,3,2,0,1:T(2,128)} copy(f32[48,4,2,24,2,48]{0,5,3,2,1,4:T(8,128)} %fusion.19) | data formatting | bytes 7077888 | tf_op jit(solution)/shard_map/kfzrx,rksby->xbfzsy/transpose | solution.py:118
  705.7 16.6 %reshape.808 = f32[48,4,4608]{2,0,1:T(8,128)} reshape(f32[48,4,2,24,2,48]{5,4,3,2,0,1:T(2,128)} %copy.163) | data formatting | bytes 7077888 | tf_op jit(solution)/shard_map/reshape | solution.py:119
  722.3 2.2 slice_bitcast_fusion.5
  724.7 44.7 %all_to_all.64 = f32[4,48,1,4608]{3,1,2,0:T(8,128)} all-to-all(f32[4,48,1,4608]{3,1,2,0:T(8,128)S(1)} %pad_maximum_fusion.1), channel_id=1, replica_groups=mesh['band'=4,'px'=4,'py'=2] {'px'}, dimensions={0} | all-to-all | bytes 7077888 | tf_op jit(solution)/shard_map/all_to_all | solution.py:35
  769.4 17.1 %reshape_reshape.7 = f32[192,2,24,2,48]{4,3,2,1,0:T(2,128)} reshape(f32[4,48,1,4608]{3,1,2,0:T(8,128)} %all_to_all.64) | data formatting | bytes 7077888 | tf_op jit(solution)/shard_map/reshape;reshape | solution.py:120
  786.5 13.2 %copy.164 = f32[192,2,24,2,48]{0,4,3,2,1:T(8,128)} copy(f32[192,2,24,2,48]{4,3,2,1,0:T(2,128)} %reshape_reshape.7) | data formatting | bytes 7077888 | tf_op jit(solution)/shard_map/reshape;reshape | solution.py:120
  799.7 10.3 fusion.9
  810.7 1.0 copy-done.2
  811.7 3.1 fusion.41
  814.8 2.6 pad_maximum_fusion
  817.4 320.4 %all-gather.2.cloned.1.call-done = f32[4,96,48,192]{3,2,1,0:T(8,128)} async-done(((f32[4,24,48,192]{3,2,1,0:T(8,128)}), f32[4,96,48,192]{3,2,1,0:T(8,128)}) %all-gather.2.cloned.1.call-update) | async-done | bytes 14155792 | tf_op jit(solution)/shard_map/all_gather | solution.py:172
  1137.8 4.8 slice_bitcast_fusion
  1142.7 11.8 %slice.55 = f32[3,96,48,192]{3,2,1,0:T(8,128)} slice(f32[4,96,48,192]{3,2,1,0:T(8,128)} %all-gather.2.cloned.1.call-done), slice={[1:4], [0:96], [0:48], [0:192]} | slice | bytes 21233664 | tf_op jit(solution)/shard_map/slice | solution.py:173
  (46 shorter events, 8.1 us)
Async XLA Ops:
  7.2 2.2 copy-start
  8.1 10.4 copy-start.5
  12.6 8.6 all-to-all-start
  192.8 45.9 %all-to-all-start.1 = ((bf16[4,2,221184]{2,1,0:T(2,128)(2,1)}), bf16[4,2,221184]{2,1,0:T(2,128)(2,1)}, u32[]{:S(2)}, u32[]{:S(2)}) async-start(bf16[4,2,221184]{2,1,0:T(2,128)(2,1)} %reshape.854), calls=%async_computation.1 | async-start | bytes 7077888 | tf_op jit(solution)/shard_map/all_to_all | solution.py:160
  197.6 176.5 %reduce-scatter.2.cloned.1.call-start = ((), (), s32[]{:S(2)}) async-start(), calls=%async_computation.7 | async-start | bytes 5898240 | tf_op jit(solution)/shard_map/reduce_scatter | solution.py:168
  398.3 25.9 %all-to-all-start.2 = ((f32[4,48,1,2304]{3,1,2,0:T(8,128)}), f32[4,48,1,2304]{3,1,2,0:T(8,128)S(1)}, u32[]{:S(2)}, u32[]{:S(2)}) async-start(f32[4,48,1,2304]{3,1,2,0:T(8,128)} %pad_maximum_fusion.2), calls=%async_computation.3 | async-start | bytes 3538944 | tf_op jit(solution)/shard_map/all_to_all | solution.py:35
  458.7 46.0 %all-to-all-start.3 = ((f32[24,8,2304]{2,0,1:T(8,128)}), f32[24,8,2304]{2,0,1:T(8,128)S(1)}, u32[]{:S(2)}, u32[]{:S(2)}) async-start(f32[24,8,2304]{2,0,1:T(8,128)} %reshape.848), calls=%async_computation.4 | async-start | bytes 3538944 | tf_op jit(solution)/shard_map/all_to_all | solution.py:43
  525.2 0.9 copy-start.3
  525.2 1.0 copy-start.4
  566.7 83.1 %all-to-all-start.4 = ((f32[24,8,4608]{2,0,1:T(8,128)}), f32[24,8,4608]{2,0,1:T(8,128)}, u32[]{:S(2)}, u32[]{:S(2)}) async-start(f32[24,8,4608]{2,0,1:T(8,128)} %reshape.849), calls=%async_computation.5 | async-start | bytes 7077888 | tf_op jit(solution)/shard_map/all_to_all | solution.py:43
  571.2 566.6 %all-gather.2.cloned.1.call-start = ((), (), s32[]{:S(2)}) async-start(), calls=%async_computation.8 | async-start | bytes 23592960 | tf_op jit(solution)/shard_map/all_gather | solution.py:172
  810.4 1.3 copy-start.2
  1142.7 11.8 %copy-start.1 = (bf16[1,128,384]{2,1,0:T(8,128)(2,1)S(1)}, bf16[1,128,384]{2,1,0:T(8,128)(2,1)}, u32[]{:S(2)}) copy-start(bf16[1,128,384]{2,1,0:T(8,128)(2,1)} %param.4) | copy-start | bytes 294916
Sparse Core Ops, SparseCore 0:
  288.9 85.1 reduce-scatter.1
  817.6 320.2 all-gather.1
